TPU v7x, 32 devices: a whole 2x2x4 slice. The times are simulated.
32 devices in a mesh: pool: 2 (over x), seq: 4 (over y, core), head: 4 (over z).
Axes of the slice: x: 2, y: 2, z: 4, core: 2. Of those that a mesh axis runs over, the one named last changes fastest.
Arguments:
- prompt: bfloat16 [8, 2048, 8192], P('pool', 'seq'), may hold values from -6 to 6
- key_value_weight: bfloat16 [8192, 2, 1024], P('seq', None, 'head'), may hold values from -0.0625 to 0.0625
- adapter_down_weight: bfloat16 [8192, 256], P('seq'), may hold values from -0.0625 to 0.0625
- adapter_up_weight: bfloat16 [8, 2, 16, 1024], P(None, None, None, 'head'), may hold values from -0.75 to 0.75
- request_adapter_index: int32 [8], P('pool'), may hold values from 0 to 7
- destination: int32 [8], replicated, may hold values from 0 to 3, as said below
- rotated_query: bfloat16 [384, 8192], P(('pool', 'seq'), 'head'), may hold values from -150 to 150
- key_value_cache: bfloat16 [384, 128, 2, 1024], P(('pool', 'seq'), None, None, 'head'), may hold values from -6 to 6
- current_key_value: bfloat16 [384, 2, 1024], P(('pool', 'seq'), None, 'head'), may hold values from -6 to 6
- cached_length: int32 [384], P(('pool', 'seq')), may hold values from 1 to 128
- row_adapter_index: int32 [384], P('pool'), may hold values from 0 to 7
- output_weight: bfloat16 [8192, 8192], P('head', 'seq'), may hold values from -0.0625 to 0.0625
- output_down_weight: bfloat16 [8192, 8, 16], P('head'), may hold values from -0.0625 to 0.0625
- output_up_weight: bfloat16 [8, 16, 8192], P(None, None, 'seq'), may hold values from -3.59375 to 3.59375
Outputs:
- handed: bfloat16 [8, 2, 2048, 2, 1024], P(('pool', 'seq'), None, None, None, 'head')
- decoded: bfloat16 [384, 8192], P(('pool', 'head'), 'seq')
Inputs may be any that keep to these rules, and one draw needn't show every extreme that they name: `destination`: among one pool's 4 requests no decode owner is named more than 2 times, and some owner exactly 2 times; in each pool owners 0 and 3 both receive requests.
All inputs are finite; a program needn't handle non-finite values.
Results may differ from a plain program's by a relative error of at most 0.0085.
Values may be sent and summed in bfloat16 or wider, within the bound.
A program may use at most 128 MiB of HBM per device.

v0:
```python
import jax
import jax.numpy as jnp
from jax import lax
from jax.sharding import PartitionSpec as P

HEAD_DIM = 128
ADAPTER_RANK = 16
ADAPTER_COUNT = 8
CAP = 2


def swapped(value, axis, distance):
    mask = 2**distance
    pairs = [(source, source ^ mask) for source in range(lax.axis_size(axis))]
    return lax.ppermute(value, axis, pairs)


def attend_local(query_matrix, key_value_cache, prefill_state, lengths):
    decode_count = query_matrix.shape[0]
    kv_heads = key_value_cache.shape[-1] // HEAD_DIM
    query_groups = query_matrix.shape[1] // HEAD_DIM // kv_heads
    positions = key_value_cache.shape[1]
    query_batch = query_matrix.reshape(decode_count, kv_heads, query_groups, HEAD_DIM)
    key_matrix = key_value_cache[:, :, 0].reshape(decode_count, positions, kv_heads, HEAD_DIM)
    value_matrix = key_value_cache[:, :, 1].reshape(decode_count, positions, kv_heads, HEAD_DIM)
    prefill_key = prefill_state[:, 0].reshape(decode_count, kv_heads, HEAD_DIM)
    prefill_value = prefill_state[:, 1].reshape(decode_count, kv_heads, HEAD_DIM)
    factor = HEAD_DIM ** (-0.5)
    scores = (
        jnp.einsum("rkgd,rckd->rkgc", query_batch, key_matrix, preferred_element_type=jnp.float32)
        * factor
    )
    own_score = (
        jnp.einsum("rkgd,rkd->rkg", query_batch, prefill_key, preferred_element_type=jnp.float32)
        * factor
    )
    valid = (jnp.arange(positions, dtype=jnp.int32)[None, :] < lengths[:, None])[:, None, None, :]
    highest = jnp.maximum(jnp.max(jnp.where(valid, scores, -1e30), axis=-1), own_score)
    raw = jnp.where(valid, jnp.exp(scores - highest[..., None]), 0.0)
    own_raw = jnp.exp(own_score - highest)
    normer = jnp.sum(raw, axis=-1) + own_raw
    weights = (raw / normer[..., None]).astype(jnp.bfloat16)
    own_weight = (own_raw / normer).astype(jnp.bfloat16)
    mixed = jnp.einsum("rkgc,rckd->rkgd", weights, value_matrix, preferred_element_type=jnp.float32)
    mixed = (
        mixed
        + own_weight.astype(jnp.float32)[..., None]
        * prefill_value.astype(jnp.float32)[:, :, None, :]
    )
    return mixed.reshape(decode_count, kv_heads * query_groups * HEAD_DIM).astype(jnp.bfloat16)


def place_slots(owner_ids, block, decoders):
    requests = block.shape[0]
    order_index = jnp.arange(requests, dtype=jnp.int32)
    same_owner = owner_ids[:, None] == owner_ids[None, :]
    slot_of = jnp.sum(
        (same_owner & (order_index[None, :] < order_index[:, None])).astype(jnp.int32), axis=1
    )
    slot_hit = slot_of[None, :] == jnp.arange(CAP, dtype=jnp.int32)[:, None]
    owner_hit = owner_ids[None, :] == jnp.arange(decoders, dtype=jnp.int32)[:, None]
    placer = (slot_hit[:, None, :] & owner_hit[None, :, :]).astype(jnp.bfloat16)
    flat = block.reshape(requests, block.shape[1] * block.shape[2] * block.shape[3])
    outgoing = jnp.einsum("cdr,rx->cdx", placer, flat, preferred_element_type=jnp.float32)
    return outgoing.astype(jnp.bfloat16).reshape(
        CAP, decoders, block.shape[1], block.shape[2], block.shape[3]
    )


def body(
    prompt,
    key_value_weight,
    adapter_down_weight,
    adapter_up_weight,
    request_adapter_index,
    destination,
    rotated_query,
    key_value_cache,
    current_key_value,
    cached_length,
    row_adapter_index,
    output_weight,
    output_down_weight,
    output_up_weight,
):
    requests, tok_dev, model_width = prompt.shape
    key_value_width = key_value_weight.shape[2]
    token_matrix = prompt.reshape(requests * tok_dev, model_width)
    weight_rows = lax.all_gather(key_value_weight, "seq", axis=0, tiled=True)
    lowered_rows = lax.all_gather(adapter_down_weight, "seq", axis=0, tiled=True)
    decode_count = weight_rows.shape[0]
    base_part = jnp.dot(
        token_matrix,
        weight_rows.reshape(decode_count, 2 * key_value_width),
        preferred_element_type=jnp.float32,
    )
    low_part = jnp.dot(token_matrix, lowered_rows, preferred_element_type=jnp.float32)
    reduced_everything = low_part
    adapter_selector = (
        request_adapter_index[:, None] == jnp.arange(ADAPTER_COUNT, dtype=jnp.int32)[None, :]
    )
    reduced_everything = reduced_everything.reshape(
        requests, tok_dev, ADAPTER_COUNT, 2, ADAPTER_RANK
    )
    low_rank = jnp.sum(
        jnp.where(adapter_selector[:, None, :, None, None], reduced_everything, 0.0), axis=2
    )
    selected_up_weight = jnp.einsum(
        "um,mdzt->udzt",
        adapter_selector.astype(jnp.bfloat16),
        adapter_up_weight,
        preferred_element_type=jnp.float32,
    )
    correction = jnp.einsum(
        "rtkq,rkqf->rtkf", low_rank, selected_up_weight, precision=lax.Precision.HIGHEST
    )
    prefilled = (base_part.reshape(requests, tok_dev, 2, key_value_width) + correction).astype(
        jnp.bfloat16
    )
    decoders = lax.axis_size("seq")
    pool_index = lax.axis_index("pool")
    other_owners = lax.dynamic_slice_in_dim(destination, (1 - pool_index) * requests, requests)
    arrived = swapped(prefilled, "pool", 0)
    outgoing = place_slots(other_owners, arrived, decoders)
    handed = lax.all_to_all(outgoing, "seq", split_axis=1, concat_axis=1, tiled=True)
    handed = handed.reshape(1, CAP, decoders * tok_dev, 2, key_value_width)
    attended = attend_local(rotated_query, key_value_cache, current_key_value, cached_length)
    down_flat = output_down_weight.reshape(
        output_down_weight.shape[0], ADAPTER_COUNT * ADAPTER_RANK
    )
    up_flat = output_up_weight.reshape(
        ADAPTER_COUNT * ADAPTER_RANK, output_up_weight.shape[2]
    ).astype(jnp.float32)
    rank_owner = jnp.arange(ADAPTER_COUNT * ADAPTER_RANK, dtype=jnp.int32) // ADAPTER_RANK
    attn_rows = lax.all_gather(attended, "seq", axis=0, tiled=True)
    low_rows = jnp.dot(attn_rows, down_flat, preferred_element_type=jnp.float32)
    low_rows = jnp.where(row_adapter_index[:, None] == rank_owner[None, :], low_rows, 0.0)
    projected = jnp.dot(attn_rows, output_weight, preferred_element_type=jnp.float32)
    terms = projected + jnp.dot(low_rows, up_flat, precision=lax.Precision.HIGHEST)
    decoded = lax.psum_scatter(terms, "head", scatter_dimension=0, tiled=True)
    return (handed, decoded.astype(jnp.bfloat16))


def solution(mesh):
    in_specs = (
        P("pool", "seq", None),
        P("seq", None, "head"),
        P("seq", None),
        P(None, None, None, "head"),
        P("pool"),
        P(),
        P(("pool", "seq"), "head"),
        P(("pool", "seq"), None, None, "head"),
        P(("pool", "seq"), None, "head"),
        P(("pool", "seq")),
        P("pool"),
        P("head", "seq"),
        P("head", None, None),
        P(None, None, "seq"),
    )
    out_specs = (P(("pool", "seq"), None, None, None, "head"), P(("pool", "head"), "seq"))
    return jax.shard_map(body, mesh=mesh, in_specs=in_specs, out_specs=out_specs, check_vma=False)
```

profile of v0, /device:TPU:0, one launch (start us, length us, event | category | flops | bytes accessed | tf_op | source)
XLA Modules:
  0.0 321.1 jit_solution(5121571751977776219)
XLA Ops:
  8.1 2.4 copy.68
  11.2 13.9 %fusion.29 = (bf16[48,128,1,256]{3,2,1,0:T(2,128)(2,1)}, bf16[48,128,1,256]{3,2,1,0:T(2,128)(2,1)}) fusion(bf16[48,128,2,256]{3,2,1,0:T(2,128)(2,1)} %param.21), kind=kLoop, calls=%fused_computation.52 | loop fusion | bytes 12582912 | tf_op jit(solution)/shard_map/slice | solution.py:24
  25.2 13.5 %copy.93 = bf16[48,128,1,256]{1,3,0,2:T(8,128)(2,1)} copy(bf16[48,128,1,256]{3,2,1,0:T(2,128)(2,1)} %get-tuple-element.8) | data formatting | bytes 6291456
  38.8 2.9 select_reduce_fusion.1
  42.9 13.6 %copy.94 = bf16[48,128,1,256]{1,3,0,2:T(8,128)(2,1)} copy(bf16[48,128,1,256]{3,2,1,0:T(2,128)(2,1)} %get-tuple-element.9) | data formatting | bytes 6291456
  56.9 4.2 %fusion.8 = bf16[48,2,8,128]{3,2,1,0:T(8,128)(2,1)S(1)} fusion(bf16[48,128,2,128]{1,3,2,0:T(8,128)(2,1)} %bitcast.84, f32[48,2,8,128]{3,2,1,0:T(8,128)S(1)} %get-tuple-element.13, f32[48,2,128]{2,1,0:T(2,128)S(1)} %bitcast.91, f32[48,2,8]{2,1,0:T(2,128)S(1)} %copy.82, f32[48,2,8]{2,1,0:T(2,128)S(1)} %copy.79, f32[48,2,8]{2,1,0:T(2,128)S(1)} %copy.77, ...), kind=kOutput, calls=%fused_computation.12 | convolution fusion | flops 25853952 | bytes 3800064 | tf_op jit(solution)/shard_map/rkgc,rckd->rkgd/dot_general | solution.py:44
  61.1 16.6 %select_reduce_fusion = f32[4,512,2,16]{1,3,2,0:T(8,128)S(1)} fusion(bf16[8,2,16,8192,1]{3,2,1,0,4:T(8,128)(2,1)} %bitcast.92, bf16[4,512,8192]{2,1,0:T(8,128)(2,1)} %param.14, pred[4,8]{1,0:T(4,128)(4,1)S(1)} %iota_compare_fusion.1), kind=kOutput, calls=%fused_computation.9 | convolution fusion | flops 8590917632 | bytes 38010912 | tf_op jit(solution)/shard_map/dot_general | solution.py:97
  77.7 29.9 %all-gather.3.cloned.1.call-done = bf16[8192,2,256]{2,1,0:T(2,128)(2,1)} async-done(((bf16[2048,2,256]{2,1,0:T(2,128)(2,1)}), bf16[8192,2,256]{2,1,0:T(2,128)(2,1)}) %all-gather.3.cloned.1.call-update) | async-done | bytes 8388624 | tf_op jit(solution)/shard_map/all_gather | solution.py:89
  107.6 21.2 %copy.92 = bf16[8192,2,256]{0,2,1:T(8,128)(2,1)} copy(bf16[8192,2,256]{2,1,0:T(2,128)(2,1)} %all-gather.3.cloned.1.call-done) | data formatting | bytes 16777216 | tf_op jit(solution)/shard_map/reshape | solution.py:94
  128.8 23.9 %fusion.2 = f32[4,512,2,256]{3,1,2,0:T(8,128)S(1)} fusion(bf16[4,512,8192]{2,1,0:T(8,128)(2,1)} %param.14, bf16[8192,2,256]{0,2,1:T(8,128)(2,1)} %copy.92), kind=kOutput, calls=%fused_computation.3 | convolution fusion | flops 17179869184 | bytes 46137344 | tf_op jit(solution)/shard_map/dot_general | solution.py:92
  152.7 4.0 %fusion.5 = bf16[4,512,2,256]{3,1,2,0:T(8,128)(2,1)S(1)} fusion(f32[4,512,2,256]{3,1,2,0:T(8,128)S(1)} %fusion.2, f32[4,512,2,16]{1,3,2,0:T(8,128)S(1)} %select_reduce_fusion, f32[4,2,16,256]{3,0,2,1:T(4,128)S(1)} %fusion.15), kind=kOutput, calls=%fused_computation.7 | convolution fusion | flops 203423744 | bytes 6684672 | tf_op jit(solution)/shard_map/rtkq,rkqf->rtkf/dot_general | solution.py:114
  158.3 8.6 %all_gather.11 = bf16[192,2048]{1,0:T(8,128)(2,1)S(1)} all-gather(bf16[48,2048]{1,0:T(8,128)(2,1)S(1)} %bitcast.87), channel_id=1, replica_groups=mesh['pool'=2,'seq'=4,'head'=4] {'seq'}, dimensions={0}, use_global_device_ids=true | all-gather | bytes 983040 | tf_op jit(solution)/shard_map/all_gather | solution.py:135
  167.2 5.2 %fusion.30 = f32[192,2048]{1,0:T(8,128)S(1)} fusion(bf16[192,2048]{1,0:T(8,128)(2,1)S(1)} %all_gather.11, bf16[2048,2048]{1,0:T(8,128)(2,1)} %param.25), kind=kOutput, calls=%fused_computation.53 | convolution fusion | flops 1610612736 | bytes 10747904 | tf_op jit(solution)/shard_map/dot_general | solution.py:138
  172.4 2.0 convolution_add_fusion
  174.7 29.9 %collective-permute-done = bf16[4,512,2,256]{3,1,2,0:T(8,128)(2,1)} collective-permute-done((bf16[4,512,2,256]{3,1,2,0:T(8,128)(2,1)S(1)}, bf16[4,512,2,256]{3,1,2,0:T(8,128)(2,1)}, u32[]{:S(2)}, u32[]{:S(2)}) %collective-permute-start) | collective-permute-done | bytes 2097184 | tf_op jit(solution)/shard_map/ppermute | solution.py:15
  204.6 5.1 %copy.71 = bf16[4,512,2,256]{3,2,1,0:T(2,128)(2,1)} copy(bf16[4,512,2,256]{3,1,2,0:T(8,128)(2,1)} %collective-permute-done) | data formatting | bytes 4194304 | tf_op jit(solution)/shard_map/ppermute | solution.py:15
  209.7 2.9 reshape.147
  212.6 3.7 %convolution_convert_fusion = bf16[2,4,262144]{2,1,0:T(4,128)(2,1)} fusion(bf16[4,262144,1]{1,0,2:T(4,128)(2,1)S(1)} %reshape.147, pred[4,4]{1,0:T(4,128)(4,1)S(1)} %iota_compare_fusion.2, pred[2,4]{1,0:T(4,128)(4,1)S(1)} %iota_compare_fusion.4), kind=kOutput, calls=%fused_computation | convolution fusion | flops 18874400 | bytes 6291480 | tf_op jit(solution)/shard_map/cdr,rx->cdx/dot_general | solution.py:64
  216.3 7.1 %reshape.136 = bf16[2,4,512,2,256]{4,3,2,1,0:T(2,128)(2,1)} reshape(bf16[2,4,262144]{2,1,0:T(4,128)(2,1)} %convolution_convert_fusion) | data formatting | bytes 8388608 | tf_op jit(solution)/shard_map/reshape | solution.py:65
  223.4 7.1 %copy.72 = bf16[2,4,512,2,256]{4,3,2,0,1:T(2,128)(2,1)} copy(bf16[2,4,512,2,256]{4,3,2,1,0:T(2,128)(2,1)} %reshape.136) | data formatting | bytes 8388608 | tf_op jit(solution)/shard_map/reshape | solution.py:65
  230.5 4.8 %all-to-all-start = ((bf16[2,4,512,2,256]{4,3,2,0,1:T(2,128)(2,1)}), bf16[2,4,512,2,256]{4,3,2,0,1:T(2,128)(2,1)}, u32[]{:S(2)}, u32[]{:S(2)}) async-start(bf16[2,4,512,2,256]{4,3,2,0,1:T(2,128)(2,1)} %copy.72), calls=%async_computation | async-start | bytes 8388608 | tf_op jit(solution)/shard_map/all_to_all | solution.py:125
  237.1 46.5 %all-to-all-done = bf16[2,4,512,2,256]{4,3,2,0,1:T(2,128)(2,1)} async-done(((bf16[2,4,512,2,256]{4,3,2,0,1:T(2,128)(2,1)}), bf16[2,4,512,2,256]{4,3,2,0,1:T(2,128)(2,1)}, u32[]{:S(2)}, u32[]{:S(2)}) %all-to-all-start) | async-done | bytes 4194336 | tf_op jit(solution)/shard_map/all_to_all | solution.py:125
  283.6 2.9 copy.73
  286.4 27.2 %copy.83 = bf16[1,2,2048,2,256]{4,3,2,1,0:T(2,128)(2,1)} copy(bf16[1,2,2048,2,256]{4,2,3,1,0:T(8,128)(2,1)S(1)} %bitcast.82) | data formatting | bytes 8388608
  (50 shorter events, 6.4 us)
Async XLA Ops:
  8.0 164.4 %copy-start = (bf16[8,16,2048]{2,1,0:T(8,128)(2,1)S(1)}, bf16[8,16,2048]{2,1,0:T(8,128)(2,1)}, u32[]{:S(2)}) copy-start(bf16[8,16,2048]{2,1,0:T(8,128)(2,1)} %param.27) | copy-start | bytes 1572868
  8.0 53.1 %all-gather.5.cloned.1.call-start = ((), (), s32[]{:S(2)}) async-start(), calls=%async_computation.3 | async-start | bytes 5242880 | tf_op jit(solution)/shard_map/all_gather | solution.py:90
  10.4 97.2 %all-gather.3.cloned.1.call-start = ((), (), s32[]{:S(2)}) async-start(), calls=%async_computation.2 | async-start | bytes 10485760 | tf_op jit(solution)/shard_map/all_gather | solution.py:89
  11.2 224.2 %reduce-scatter.2.cloned.1.call-start = ((), (), s32[]{:S(2)}) async-start(), calls=%async_computation.4 | async-start | bytes 1966080 | tf_op jit(solution)/shard_map/reduce_scatter | solution.py:140
  25.1 13.6 %copy-start.2 = (bf16[48,2048]{1,0:T(8,128)(2,1)S(1)}, bf16[48,2048]{1,0:T(8,128)(2,1)}, u32[]{:S(2)}) copy-start(bf16[48,2048]{1,0:T(8,128)(2,1)} %param.20) | copy-start | bytes 589828
  25.1 13.6 %copy-start.7 = (s32[48]{0:T(128)S(1)}, s32[48]{0:T(128)}, u32[]{:S(2)}) copy-start(s32[48]{0:T(128)} %param.23) | copy-start | bytes 580
  38.7 3.1 copy-start.4
  42.9 13.6 %copy-start.6 = (s32[4]{0:T(128)S(1)}, s32[4]{0:T(128)}, u32[]{:S(2)}) copy-start(s32[4]{0:T(128)} %param.18) | copy-start | bytes 52
  42.9 13.7 %copy-start.3 = (bf16[8,2,16,256]{3,2,1,0:T(8,128)(2,1)S(1)}, bf16[8,2,16,256]{3,2,1,0:T(8,128)(2,1)}, u32[]{:S(2)}) copy-start(bf16[8,2,16,256]{3,2,1,0:T(8,128)(2,1)} %param.17) | copy-start | bytes 393220
  152.7 14.1 %copy-start.1 = (bf16[2048,8,16]{0,2,1:T(8,128)(2,1)S(1)}, bf16[2048,8,16]{0,2,1:T(8,128)(2,1)}, u32[]{:S(2)}) copy-start(bf16[2048,8,16]{0,2,1:T(8,128)(2,1)} %param.26) | copy-start | bytes 1572868
  152.7 14.1 %copy-start.5 = (s32[192]{0:T(256)S(1)}, s32[192]{0:T(256)}, u32[]{:S(2)}) copy-start(s32[192]{0:T(256)} %param.24) | copy-start | bytes 2308
  156.7 47.9 %collective-permute-start = (bf16[4,512,2,256]{3,1,2,0:T(8,128)(2,1)S(1)}, bf16[4,512,2,256]{3,1,2,0:T(8,128)(2,1)}, u32[]{:S(2)}, u32[]{:S(2)}) collective-permute-start(bf16[4,512,2,256]{3,1,2,0:T(8,128)(2,1)S(1)} %fusion.5), channel_id=1, source_target_pairs={{0,16},{16,0},{1,17},{17,1},{2,18},{18,2},{3,19},{19,3},{4,20},{20... | collective-permute-start | bytes 6291464 | tf_op jit(solution)/shard_map/ppermute | solution.py:15
  172.4 2.0 copy-start.8
  230.5 53.0 %all-to-all-start = ((bf16[2,4,512,2,256]{4,3,2,0,1:T(2,128)(2,1)}), bf16[2,4,512,2,256]{4,3,2,0,1:T(2,128)(2,1)}, u32[]{:S(2)}, u32[]{:S(2)}) async-start(bf16[2,4,512,2,256]{4,3,2,0,1:T(2,128)(2,1)} %copy.72), calls=%async_computation | async-start | bytes 8388608 | tf_op jit(solution)/shard_map/all_to_all | solution.py:125
Sparse Core Ops, SparseCore 0:
  10.6 37.1 all-gather.4
  49.3 58.2 all-gather.2
Sparse Core Ops, SparseCore 1:
  174.5 34.7 reduce-scatter.1
where the time goes:
time: 323 us; the launch traced here: 321 us
  local copies, waits for them, and re-layouts  118 us (37%)
  waiting for transfers between devices  107 us (33%)
  matrix products  63.3 us (20%)
  between operations  15.7 us (5%)
  blocking collectives  8.55 us (3%)
  starting transfers between devices  6.5 us (2%)
    unnamed x24, local copies, waits for them, and re-layouts  56.8 us
    all_to_all x1, waiting for transfers between devices, body(): lax.all_to_all(outgoing, 'seq', split_axis=1, concat_axis=1, tiled=True)  46.5 us
    all_gather x1, waiting for transfers between devices, body(): weight_rows = lax.all_gather(key_value_weight, 'seq', axis=0, tiled=True)  29.9 us
    ppermute x1, waiting for transfers between devices, swapped(): return lax.ppermute(value, axis, pairs)  29.9 us
    dot_general x1, matrix products, body(): jnp.dot(token_matrix, weight_rows.reshape(decode_count, 2 * key_value_wid...  23.9 us
    reshape x1, local copies, waits for them, and re-layouts, body(): weight_rows.reshape(decode_count, 2 * key_value_width)  21.2 us
    dot_general x1, matrix products, body(): jnp.dot(token_matrix, lowered_rows, preferred_element_type=jnp.float32)  16.6 us
    reshape x2, local copies, waits for them, and re-layouts, place_slots(): outgoing.astype(jnp.bfloat16)  14.2 us
  transfers between devices with their start and end apart: 5, of which 3 were waited for; matrix products, arithmetic and copies ran while one was open for 32% of the time, Pallas kernels for 0%

commit v1 on v0

--- a/solution.py
+++ b/solution.py
@@ -2,6 +2,7 @@
 import jax.numpy as jnp
 from jax import lax
 from jax.sharding import PartitionSpec as P
+from jax.lax import all_to_all, axis_size
 
 HEAD_DIM = 128
 ADAPTER_RANK = 16
@@ -122,7 +123,9 @@
     other_owners = lax.dynamic_slice_in_dim(destination, (1 - pool_index) * requests, requests)
     arrived = swapped(prefilled, "pool", 0)
     outgoing = place_slots(other_owners, arrived, decoders)
-    handed = lax.all_to_all(outgoing, "seq", split_axis=1, concat_axis=1, tiled=True)
+    handed = jnp.concatenate(
+        all_to_all(jnp.stack(jnp.split(outgoing, axis_size("seq"), 1), axis=0), "seq", 0, 0), 1
+    )
     handed = handed.reshape(1, CAP, decoders * tok_dev, 2, key_value_width)
     attended = attend_local(rotated_query, key_value_cache, current_key_value, cached_length)
     down_flat = output_down_weight.reshape(

time: 323 us -> 306 us (0.947)
  local copies, waits for them, and re-layouts: 118 us -> 91.9 us
  other arithmetic: 2.48 us -> 11 us
    unnamed x24 -> x23, local copies, waits for them, and re-layouts: 56.8 us -> 29.6 us
    another operation x0 -> x1, other arithmetic: none -> 8.55 us  [body(): jnp.stack(jnp.split(outgoing, axis_size('seq'), 1), axis=0)]
    reshape x0 -> x1, local copies, waits for them, and re-layouts: none -> 7.08 us  [body(): jnp.concatenate(all_to_all(jnp.stack(jnp.split(outgoing, axis_size('seq')...]
    reshape x2 -> x1, local copies, waits for them, and re-layouts: 14.2 us -> 7.12 us  [place_slots(): outgoing.astype(jnp.bfloat16)]
    another operation x0 -> x1, local copies, waits for them, and re-layouts: none -> 4.43 us  [body(): jnp.stack(jnp.split(outgoing, axis_size('seq'), 1), axis=0)]
  transfers between devices with their start and end apart: 5 -> 5, of which waited for: 3 -> 3; matrix products, arithmetic and copies ran while one was open for 32% -> 35% of each run, Pallas kernels for 0% -> 0%
where the time goes in v1:
time: 306 us; the launch traced here: 304 us
  waiting for transfers between devices  107 us (35%)
  local copies, waits for them, and re-layouts  91.9 us (30%)
  matrix products  63.2 us (21%)
  between operations  15.7 us (5%)
  other arithmetic  11 us (4%)
  blocking collectives  8.55 us (3%)
  starting transfers between devices  6.51 us (2%)
    all_to_all x1, waiting for transfers between devices, body(): all_to_all(jnp.stack(jnp.split(outgoing, axis_size('seq'), 1), axis=0), '...  46.5 us
    ppermute x1, waiting for transfers between devices, swapped(): return lax.ppermute(value, axis, pairs)  29.9 us
    all_gather x1, waiting for transfers between devices, body(): weight_rows = lax.all_gather(key_value_weight, 'seq', axis=0, tiled=True)  29.9 us
    unnamed x23, local copies, waits for them, and re-layouts  29.6 us
    dot_general x1, matrix products, body(): jnp.dot(token_matrix, weight_rows.reshape(decode_count, 2 * key_value_wid...  23.9 us
    reshape x1, local copies, waits for them, and re-layouts, body(): weight_rows.reshape(decode_count, 2 * key_value_width)  21.2 us
    dot_general x1, matrix products, body(): jnp.dot(token_matrix, lowered_rows, preferred_element_type=jnp.float32)  16.6 us
    slice x1, local copies, waits for them, and re-layouts, attend_local(): key_value_cache[:, :, 0]  13.9 us
  transfers between devices with their start and end apart: 5, of which 3 were waited for; matrix products, arithmetic and copies ran while one was open for 35% of the time, Pallas kernels for 0%

profile of v1, /device:TPU:0, one launch (start us, length us, event | category | flops | bytes accessed | tf_op | source)
XLA Modules:
  0.0 304.1 jit_solution(4150813999843720291)
XLA Ops:
  8.1 2.4 copy.67
  11.3 13.9 %fusion.29 = (bf16[48,128,1,256]{3,2,1,0:T(2,128)(2,1)}, bf16[48,128,1,256]{3,2,1,0:T(2,128)(2,1)}) fusion(bf16[48,128,2,256]{3,2,1,0:T(2,128)(2,1)} %param.21), kind=kLoop, calls=%fused_computation.57 | loop fusion | bytes 12582912 | tf_op jit(solution)/shard_map/slice | solution.py:25
  25.2 13.5 %copy.96 = bf16[48,128,1,256]{1,3,0,2:T(8,128)(2,1)} copy(bf16[48,128,1,256]{3,2,1,0:T(2,128)(2,1)} %get-tuple-element.2) | data formatting | bytes 6291456
  38.8 2.9 select_reduce_fusion.1
  42.9 13.6 %copy.97 = bf16[48,128,1,256]{1,3,0,2:T(8,128)(2,1)} copy(bf16[48,128,1,256]{3,2,1,0:T(2,128)(2,1)} %get-tuple-element.3) | data formatting | bytes 6291456
  56.9 4.2 %fusion.8 = bf16[48,2,8,128]{3,2,1,0:T(8,128)(2,1)S(1)} fusion(bf16[48,128,2,128]{1,3,2,0:T(8,128)(2,1)} %bitcast.99, f32[48,2,8,128]{3,2,1,0:T(8,128)S(1)} %get-tuple-element.11, f32[48,2,128]{2,1,0:T(2,128)S(1)} %bitcast.106, f32[48,2,8]{2,1,0:T(2,128)S(1)} %copy.83, f32[48,2,8]{2,1,0:T(2,128)S(1)} %copy.80, f32[48,2,8]{2,1,0:T(2,128)S(1)} %copy.78, ...), kind=kOutput, calls=%fused_computation.13 | convolution fusion | flops 25853952 | bytes 3800064 | tf_op jit(solution)/shard_map/rkgc,rckd->rkgd/dot_general | solution.py:45
  61.1 16.6 %select_reduce_fusion = f32[4,512,2,16]{1,3,2,0:T(8,128)S(1)} fusion(bf16[8,2,16,8192,1]{3,2,1,0,4:T(8,128)(2,1)} %bitcast.107, bf16[4,512,8192]{2,1,0:T(8,128)(2,1)} %param.14, pred[4,8]{1,0:T(4,128)(4,1)S(1)} %iota_compare_fusion.1), kind=kOutput, calls=%fused_computation.10 | convolution fusion | flops 8590917632 | bytes 38010912 | tf_op jit(solution)/shard_map/dot_general | solution.py:98
  77.7 29.9 %all-gather.3.cloned.1.call-done = bf16[8192,2,256]{2,1,0:T(2,128)(2,1)} async-done(((bf16[2048,2,256]{2,1,0:T(2,128)(2,1)}), bf16[8192,2,256]{2,1,0:T(2,128)(2,1)}) %all-gather.3.cloned.1.call-update) | async-done | bytes 8388624 | tf_op jit(solution)/shard_map/all_gather | solution.py:90
  107.6 21.2 %copy.92 = bf16[8192,2,256]{0,2,1:T(8,128)(2,1)} copy(bf16[8192,2,256]{2,1,0:T(2,128)(2,1)} %all-gather.3.cloned.1.call-done) | data formatting | bytes 16777216 | tf_op jit(solution)/shard_map/reshape | solution.py:95
  128.8 23.9 %fusion.2 = f32[4,512,2,256]{3,1,2,0:T(8,128)S(1)} fusion(bf16[4,512,8192]{2,1,0:T(8,128)(2,1)} %param.14, bf16[8192,2,256]{0,2,1:T(8,128)(2,1)} %copy.92), kind=kOutput, calls=%fused_computation.3 | convolution fusion | flops 17179869184 | bytes 46137344 | tf_op jit(solution)/shard_map/dot_general | solution.py:93
  152.8 3.9 %fusion.5 = bf16[4,512,2,256]{3,1,2,0:T(8,128)(2,1)S(1)} fusion(f32[4,512,2,256]{3,1,2,0:T(8,128)S(1)} %fusion.2, f32[4,512,2,16]{1,3,2,0:T(8,128)S(1)} %select_reduce_fusion, f32[4,2,16,256]{3,0,2,1:T(4,128)S(1)} %fusion.15), kind=kOutput, calls=%fused_computation.8 | convolution fusion | flops 203423744 | bytes 6684672 | tf_op jit(solution)/shard_map/rtkq,rkqf->rtkf/dot_general | solution.py:115
  158.3 8.5 %all_gather.11 = bf16[192,2048]{1,0:T(8,128)(2,1)S(1)} all-gather(bf16[48,2048]{1,0:T(8,128)(2,1)S(1)} %bitcast.102), channel_id=1, replica_groups=mesh['pool'=2,'seq'=4,'head'=4] {'seq'}, dimensions={0}, use_global_device_ids=true | all-gather | bytes 983040 | tf_op jit(solution)/shard_map/all_gather | solution.py:138
  167.2 5.2 %fusion.30 = f32[192,2048]{1,0:T(8,128)S(1)} fusion(bf16[192,2048]{1,0:T(8,128)(2,1)S(1)} %all_gather.11, bf16[2048,2048]{1,0:T(8,128)(2,1)} %param.25), kind=kOutput, calls=%fused_computation.58 | convolution fusion | flops 1610612736 | bytes 10747904 | tf_op jit(solution)/shard_map/dot_general | solution.py:141
  172.5 2.0 convolution_add_fusion
  174.8 29.9 %collective-permute-done = bf16[4,512,2,256]{3,1,2,0:T(8,128)(2,1)} collective-permute-done((bf16[4,512,2,256]{3,1,2,0:T(8,128)(2,1)S(1)}, bf16[4,512,2,256]{3,1,2,0:T(8,128)(2,1)}, u32[]{:S(2)}, u32[]{:S(2)}) %collective-permute-start) | collective-permute-done | bytes 2097184 | tf_op jit(solution)/shard_map/ppermute | solution.py:16
  204.7 5.1 %copy.70 = bf16[4,512,2,256]{3,2,1,0:T(2,128)(2,1)} copy(bf16[4,512,2,256]{3,1,2,0:T(8,128)(2,1)} %collective-permute-done) | data formatting | bytes 4194304 | tf_op jit(solution)/shard_map/ppermute | solution.py:16
  209.8 2.9 reshape.147
  212.7 3.7 %convolution_convert_fusion = bf16[2,4,262144]{2,1,0:T(4,128)(2,1)} fusion(bf16[4,262144,1]{1,0,2:T(4,128)(2,1)S(1)} %reshape.147, pred[4,4]{1,0:T(4,128)(4,1)S(1)} %iota_compare_fusion.2, pred[2,4]{1,0:T(4,128)(4,1)S(1)} %iota_compare_fusion.4), kind=kOutput, calls=%fused_computation | convolution fusion | flops 18874400 | bytes 6291480 | tf_op jit(solution)/shard_map/cdr,rx->cdx/dot_general | solution.py:65
  216.4 7.1 %reshape.136 = bf16[2,4,512,2,256]{4,3,2,1,0:T(2,128)(2,1)} reshape(bf16[2,4,262144]{2,1,0:T(4,128)(2,1)} %convolution_convert_fusion) | data formatting | bytes 8388608 | tf_op jit(solution)/shard_map/reshape | solution.py:66
  223.5 4.4 %slice_bitcast_fusion.3 = (bf16[1,2,1,512,2,256]{5,4,3,1,2,0:T(2,128)(2,1)S(1)}, bf16[1,2,1,512,2,256]{5,4,3,1,2,0:T(2,128)(2,1)S(1)}, bf16[1,2,1,512,2,256]{5,4...) fusion(bf16[2,4,512,2,256]{4,3,2,1,0:T(2,128)(2,1)} %reshape.136), kind=kLoop, calls=%fused_computation.18 | loop fusion | bytes 8388608 | tf_op jit(solution)/shard_map/stack | solution.py:127
  227.9 8.6 %pad_maximum_fusion = bf16[4,2,1,512,2,256]{5,4,3,1,2,0:T(2,128)(2,1)} fusion(bf16[1,2,1,512,2,256]{5,4,3,1,2,0:T(2,128)(2,1)S(1)} %get-tuple-element.6, bf16[1,2,1,512,2,256]{5,4,3,1,2,0:T(2,128)(2,1)S(1)} %get-tuple-element.7, bf16[1,2,1,512,2,256]{5,4,3,1,2,0:T(2,128)(2,1)S(1)} %get-tuple-element.5, bf16[1,2,1,512,2,256]{5,4,3,1,2,0:T(2,128)(2,1)S(1)} %get-tuple-element.4), kind=kLoop, calls=%fused_computation.6 | loop fusion | flops 6291456 | bytes 8388608 | tf_op jit(solution)/shard_map/stack | solution.py:127
  236.5 4.8 %all-to-all-start = ((bf16[4,2,1,512,2,256]{5,4,3,1,2,0:T(2,128)(2,1)}), bf16[4,2,1,512,2,256]{5,4,3,1,2,0:T(2,128)(2,1)}, u32[]{:S(2)}, u32[]{:S(2)}) async-start(bf16[4,2,1,512,2,256]{5,4,3,1,2,0:T(2,128)(2,1)} %pad_maximum_fusion), calls=%async_computation | async-start | bytes 8388608 | tf_op jit(solution)/shard_map/all_to_all | solution.py:127
  243.1 46.5 %all-to-all-done = bf16[4,2,1,512,2,256]{5,4,3,1,2,0:T(2,128)(2,1)} async-done(((bf16[4,2,1,512,2,256]{5,4,3,1,2,0:T(2,128)(2,1)}), bf16[4,2,1,512,2,256]{5,4,3,1,2,0:T(2,128)(2,1)}, u32[]{:S(2)}, u32[]{:S(2)}) %all-to-all-start) | async-done | bytes 4194336 | tf_op jit(solution)/shard_map/all_to_all | solution.py:127
  289.5 7.1 %copy.74 = bf16[2,4,1,512,2,256]{5,4,3,1,0,2:T(2,128)(2,1)} copy(bf16[2,4,1,512,2,256]{5,4,3,0,2,1:T(2,128)(2,1)} %bitcast.18) | data formatting | bytes 8388608 | tf_op jit(solution)/shard_map/reshape | solution.py:126
  (50 shorter events, 6.5 us)
Async XLA Ops:
  8.0 164.4 %copy-start = (bf16[8,16,2048]{2,1,0:T(8,128)(2,1)S(1)}, bf16[8,16,2048]{2,1,0:T(8,128)(2,1)}, u32[]{:S(2)}) copy-start(bf16[8,16,2048]{2,1,0:T(8,128)(2,1)} %param.27) | copy-start | bytes 1572868
  8.0 53.1 %all-gather.5.cloned.1.call-start = ((), (), s32[]{:S(2)}) async-start(), calls=%async_computation.3 | async-start | bytes 5242880 | tf_op jit(solution)/shard_map/all_gather | solution.py:91
  10.5 97.2 %all-gather.3.cloned.1.call-start = ((), (), s32[]{:S(2)}) async-start(), calls=%async_computation.2 | async-start | bytes 10485760 | tf_op jit(solution)/shard_map/all_gather | solution.py:90
  11.2 230.2 %reduce-scatter.2.cloned.1.call-start = ((), (), s32[]{:S(2)}) async-start(), calls=%async_computation.4 | async-start | bytes 1966080 | tf_op jit(solution)/shard_map/reduce_scatter | solution.py:143
  25.1 13.6 %copy-start.2 = (bf16[48,2048]{1,0:T(8,128)(2,1)S(1)}, bf16[48,2048]{1,0:T(8,128)(2,1)}, u32[]{:S(2)}) copy-start(bf16[48,2048]{1,0:T(8,128)(2,1)} %param.20) | copy-start | bytes 589828
  25.1 13.6 %copy-start.7 = (s32[48]{0:T(128)S(1)}, s32[48]{0:T(128)}, u32[]{:S(2)}) copy-start(s32[48]{0:T(128)} %param.23) | copy-start | bytes 580
  38.7 3.1 %copy-start.4 = (bf16[48,2,256]{2,1,0:T(2,128)(2,1)S(1)}, bf16[48,2,256]{2,1,0:T(2,128)(2,1)}, u32[]{:S(2)}) copy-start(bf16[48,2,256]{2,1,0:T(2,128)(2,1)} %param.22) | copy-start | bytes 147460
  42.9 13.6 %copy-start.6 = (s32[4]{0:T(128)S(1)}, s32[4]{0:T(128)}, u32[]{:S(2)}) copy-start(s32[4]{0:T(128)} %param.18) | copy-start | bytes 52
  42.9 13.7 %copy-start.3 = (bf16[8,2,16,256]{3,2,1,0:T(8,128)(2,1)S(1)}, bf16[8,2,16,256]{3,2,1,0:T(8,128)(2,1)}, u32[]{:S(2)}) copy-start(bf16[8,2,16,256]{3,2,1,0:T(8,128)(2,1)} %param.17) | copy-start | bytes 393220
  152.7 14.1 %copy-start.1 = (bf16[2048,8,16]{0,2,1:T(8,128)(2,1)S(1)}, bf16[2048,8,16]{0,2,1:T(8,128)(2,1)}, u32[]{:S(2)}) copy-start(bf16[2048,8,16]{0,2,1:T(8,128)(2,1)} %param.26) | copy-start | bytes 1572868
  152.8 14.1 %copy-start.5 = (s32[192]{0:T(256)S(1)}, s32[192]{0:T(256)}, u32[]{:S(2)}) copy-start(s32[192]{0:T(256)} %param.24) | copy-start | bytes 2308
  156.7 48.0 %collective-permute-start = (bf16[4,512,2,256]{3,1,2,0:T(8,128)(2,1)S(1)}, bf16[4,512,2,256]{3,1,2,0:T(8,128)(2,1)}, u32[]{:S(2)}, u32[]{:S(2)}) collective-permute-start(bf16[4,512,2,256]{3,1,2,0:T(8,128)(2,1)S(1)} %fusion.5), channel_id=1, source_target_pairs={{0,16},{16,0},{1,17},{17,1},{2,18},{18,2},{3,19},{19,3},{4,20},{20... | collective-permute-start | bytes 6291464 | tf_op jit(solution)/shard_map/ppermute | solution.py:16
  172.5 2.0 copy-start.8
  236.5 53.1 %all-to-all-start = ((bf16[4,2,1,512,2,256]{5,4,3,1,2,0:T(2,128)(2,1)}), bf16[4,2,1,512,2,256]{5,4,3,1,2,0:T(2,128)(2,1)}, u32[]{:S(2)}, u32[]{:S(2)}) async-start(bf16[4,2,1,512,2,256]{5,4,3,1,2,0:T(2,128)(2,1)} %pad_maximum_fusion), calls=%async_computation | async-start | bytes 8388608 | tf_op jit(solution)/shard_map/all_to_all | solution.py:127
Sparse Core Ops, SparseCore 0:
  10.6 37.1 all-gather.4
  49.3 58.2 all-gather.2
Sparse Core Ops, SparseCore 1:
  174.5 34.7 reduce-scatter.1
